TPU v7x, 128 devices: a whole 4x4x4 slice. The times are simulated.
128 devices in a mesh: row: 4 (over y), col: 32 (over z, x, core).
Axes of the slice: x: 4, y: 4, z: 4, core: 2. Of those that a mesh axis runs over, the one named last changes fastest.
Arguments:
- node_features: bfloat16 [8192, 128, 512], P(('row', 'col')), may hold values from -6 to 6
- node_counts: int32 [8192], P(('row', 'col')), may hold values from 16 to 128, as said below
- edge_list: int32 [8192, 2, 256], P(('row', 'col')), may hold values from 0 to 128, as said below
- readout_ids: int32 [8192], P(('row', 'col')), may hold values from 0 to 1023
- live_graphs: int32 [128], P(('row', 'col')), may hold values from 1 to 64, as said below
- self_weight: float32 [1], replicated, may hold values from 0.5 to 1.5
- w_first: bfloat16 [512, 512], replicated, may hold values from -0.25 to 0.25
- b_first: float32 [512], replicated, may hold values from -3 to 3
- w_second: bfloat16 [512, 512], replicated, may hold values from -0.25 to 0.25
- b_second: float32 [512], replicated, may hold values from -3 to 3
- w_third: bfloat16 [512, 512], replicated, may hold values from -0.25 to 0.25
- b_third: float32 [512], replicated, may hold values from -3 to 3
Outputs:
- node_out: bfloat16 [4096, 128, 512], P(('row', 'col'))
- readout: float32 [1024, 512], P(('row', 'col'))
Inputs may be any that keep to these rules, and one draw needn't show every extreme that they name: `live_graphs`: the entries sum to 4096, and at least one equals 64. `node_counts`: node slots 0 to count - 1 of a graph are live; the rest of its block is padding. `edge_list`: each edge slot holds two node indices below its graph's node count, or 128 in both rows for an unused slot.
All inputs are finite; a program needn't handle non-finite values.
Results may differ from a plain program's by a relative error of at most 0.0058.
Values may be sent and summed in bfloat16 or wider, within the bound.
No kernel may reach another device: no remote copies, remote signals or barrier semaphores. Data moves between devices by JAX's collectives and lax.ppermute only.
A program may use at most 128 MiB of HBM per device.

v0:
```python
import jax
import jax.numpy as jnp
from jax import lax
from jax.sharding import Mesh
from jax.sharding import PartitionSpec as P

G_DEV = 32
READ_DEV = 8
ROW_COL = ("row", "col_0", "col_1", "col_2")


def sent_to_all(x, axis):
    copies = jnp.broadcast_to(x, (lax.axis_size(axis), *x.shape))
    return lax.all_to_all(copies, axis, split_axis=0, concat_axis=0, tiled=True)


def in_order(parts, dim):
    shape = list(parts.shape[1:])
    shape[dim] *= parts.shape[0]
    return jnp.moveaxis(parts, 0, dim).reshape(shape)


def whole_of(x, axes, dim):
    far, near = axes
    parts = sent_to_all(sent_to_all(x, far), near)
    return in_order(parts.swapaxes(0, 1).reshape(-1, *x.shape), dim)


def cut_along(x, dim, count):
    before, after = (x.shape[:dim], x.shape[dim + 1 :])
    return jnp.moveaxis(x.reshape(*before, count, -1, *after), dim, 0)


def summed_on_arrival(x, axis, dim):
    count = lax.axis_size(axis)
    parts = lax.all_to_all(cut_along(x, dim, count), axis, 0, 0, tiled=True)
    return jnp.sum(parts.astype(jnp.float32), axis=0)


def sum_by_axis(x, axes, dim):
    far, near = axes
    own = summed_on_arrival(cut_along(x, dim, lax.axis_size(far)), near, dim + 1)
    return jnp.sum(
        lax.all_to_all(own.astype(jnp.bfloat16), far, 0, 0, tiled=True).astype(jnp.float32), axis=0
    )


def blend_nodes(features, edge_slots, self_weight):
    node_index = lax.broadcasted_iota(jnp.int32, (1, 1, features.shape[1]), 2)
    sources = (edge_slots[:, 0, :, None] == node_index).astype(jnp.bfloat16)
    targets = (edge_slots[:, 1, :, None] == node_index).astype(jnp.bfloat16)
    adjacency = jnp.einsum(
        "gek,gel->gkl", targets, sources, preferred_element_type=jnp.float32
    ).astype(jnp.bfloat16)
    neighbour = jnp.einsum("gkl,glh->gkh", adjacency, features, preferred_element_type=jnp.float32)
    return (self_weight[0] * features.astype(jnp.float32) + neighbour).astype(jnp.bfloat16)


def perceptron(blended, weights):
    w_first, b_first, w_second, b_second, w_third, b_third = weights
    flat_rows = blended.reshape(-1, blended.shape[-1])
    hidden_one = jax.nn.relu(
        jnp.dot(flat_rows, w_first, preferred_element_type=jnp.float32) + b_first
    ).astype(jnp.bfloat16)
    hidden_two = jax.nn.relu(
        jnp.dot(hidden_one, w_second, preferred_element_type=jnp.float32) + b_second
    ).astype(jnp.bfloat16)
    result = jnp.dot(hidden_two, w_third, preferred_element_type=jnp.float32) + b_third
    return result.reshape(blended.shape)


def arrival_index(slot_tags):
    wanted = lax.broadcasted_iota(jnp.int32, (G_DEV, slot_tags.shape[0]), 0)
    places = lax.broadcasted_iota(jnp.int32, (G_DEV, slot_tags.shape[0]), 1)
    return jnp.sum(jnp.where(slot_tags[None, :] == wanted, places, 0), axis=1)


def readout_terms(graph_ids, pooled, row_count):
    id_keys = lax.broadcasted_iota(jnp.int32, (row_count, graph_ids.shape[0]), 0)
    members = (id_keys == graph_ids[None, :]).astype(jnp.float32)
    return jnp.dot(
        members, pooled, precision=lax.Precision.HIGHEST, preferred_element_type=jnp.float32
    )


def body(
    node_features,
    node_counts,
    edge_list,
    readout_ids,
    live_graphs,
    self_weight,
    w_first,
    b_first,
    w_second,
    b_second,
    w_third,
    b_third,
):
    weights = (w_first, b_first, w_second, b_second, w_third, b_third)
    devices = lax.axis_size(ROW_COL)
    capacity = node_features.shape[0]
    bucket = (capacity + devices - 1) // devices
    own_count = live_graphs[0]
    every_count = whole_of(live_graphs, (("row", "col_0", "col_1"), "col_2"), 0)
    position = lax.broadcasted_iota(jnp.int32, (devices,), 0)
    offset = jnp.sum(jnp.where(position < lax.axis_index(ROW_COL), every_count, 0))
    targets = lax.broadcasted_iota(jnp.int32, (devices * bucket,), 0)
    dest_device = targets // bucket
    within = (dest_device - offset) % devices + targets % bucket * devices
    sending_ok = within < own_count
    slot_tags = jnp.where(sending_ok, (offset + within) // devices, G_DEV)
    picked = jnp.minimum(within, capacity - 1)
    node_index = lax.broadcasted_iota(jnp.int32, (1, node_features.shape[1]), 1)
    blended = blend_nodes(node_features, edge_list, self_weight)
    live_nodes = node_index < node_counts[:, None]
    results = jnp.where(live_nodes[:, :, None], perceptron(blended, weights), 0.0).astype(
        jnp.bfloat16
    )
    pooled = jnp.sum(results.astype(jnp.float32), axis=1) / node_counts[:, None].astype(jnp.float32)
    slot_live = lax.broadcasted_iota(jnp.int32, (capacity,), 0) < own_count
    graph_ids = jnp.where(slot_live, readout_ids, -1)
    arrived, arrived_tags = (
        lax.all_to_all(results[picked], ROW_COL, split_axis=0, concat_axis=0, tiled=True),
        lax.all_to_all(slot_tags, ROW_COL, split_axis=0, concat_axis=0, tiled=True),
    )
    node_out = arrived[arrival_index(arrived_tags)]
    readout = sum_by_axis(
        readout_terms(graph_ids, pooled, READ_DEV * lax.axis_size(ROW_COL)).astype(jnp.bfloat16),
        (("row", "col_0", "col_1"), "col_2"),
        0,
    )
    return (node_out, readout)


def solution(mesh):
    split = Mesh(
        mesh.devices.reshape(mesh.shape["row"], 4, 4, 2), ("row", "col_0", "col_1", "col_2")
    )
    return jax.shard_map(
        body,
        mesh=split,
        in_specs=(
            P(ROW_COL, None, None),
            P(ROW_COL),
            P(ROW_COL, None, None),
            P(ROW_COL),
            P(ROW_COL),
            P(),
            P(),
            P(),
            P(),
            P(),
            P(),
            P(),
        ),
        out_specs=(P(ROW_COL, None, None), P(ROW_COL, None)),
        check_vma=False,
    )
```

profile of v0, /device:TPU:0, one launch (start us, length us, event | category | flops | bytes accessed | tf_op | source)
XLA Modules:
  0.0 360.8 jit_solution(12937163495116750141)
XLA Ops:
  2.0 11.5 %all-to-all-start = ((s32[64,1,1]{2,1,0:T(1,128)}), s32[64,1,1]{2,1,0:T(1,128)S(1)}, u32[]{:S(2)}, u32[]{:S(2)}) async-start(s32[64,1,1]{2,1,0:T(1,128)} %broadcast_in_dim.43), calls=%async_computation | async-start | bytes 65536 | tf_op jit(solution)/shard_map/all_to_all | solution.py:14
  14.2 0.7 iota_compare_fusion.14
  15.6 1.1 fusion.14
  17.3 12.6 %add_convert_fusion = bf16[64,128,512]{2,1,0:T(8,128)(2,1)} fusion(bf16[64,128,512]{2,1,0:T(8,128)(2,1)} %param.12, f32[]{:T(128)} %bitcast.32, s32[64,256]{1,0:T(8,128)S(1)} %get-tuple-element.6, s32[64,256]{1,0:T(8,128)S(1)} %get-tuple-element.7), kind=kOutput, calls=%fused_computation.6 | convolution fusion | flops 1632632832 | bytes 16908292 | tf_op jit(solution)/shard_map/gkl,glh->gkh/dot_general | solution.py:55
  30.0 10.2 %maximum_convert_fusion.1 = bf16[8192,512]{1,0:T(8,128)(2,1)} fusion(bf16[8192,512]{1,0:T(8,128)(2,1)} %bitcast.34, bf16[512,512]{1,0:T(8,128)(2,1)S(1)} %copy-done, f32[512]{0:T(512)S(1)} %copy-done.4), kind=kOutput, calls=%fused_computation.5 | convolution fusion | flops 4307550208 | bytes 17303552 | tf_op jit(solution)/shard_map/dot_general | solution.py:63
  40.2 13.2 %convolution_add_fusion = bf16[8192,512]{1,0:T(8,128)(2,1)} fusion(bf16[512,512]{1,0:T(8,128)(2,1)S(1)} %copy-done.2, f32[512]{0:T(512)S(1)} %copy-done.5, bf16[8192,512]{1,0:T(8,128)(2,1)} %maximum_convert_fusion.1, bf16[512,512]{1,0:T(8,128)(2,1)S(1)} %copy-done.3, f32[512]{0:T(512)S(1)} %copy-done.6), kind=kOutput, calls=%fused_computation.7 | convolution fusion | flops 8610906112 | bytes 17829888 | tf_op jit(solution)/shard_map/dot_general | solution.py:68
  53.5 8.3 %convert_reduce_fusion = (f32[64,512]{1,0:T(8,128)S(1)}, bf16[64,128,512]{2,1,0:T(8,128)(2,1)}) fusion(pred[64,128]{1,0:T(8,128)(4,1)S(1)} %iota_compare_fusion.14, bf16[8192,512]{1,0:T(8,128)(2,1)} %convolution_add_fusion), kind=kLoop, calls=%fused_computation.2 | loop fusion | flops 12550144 | bytes 16916480 | tf_op jit(solution)/shard_map/reduce_sum | solution.py:120
  61.8 1.1 convolution_convert_fusion
  62.9 1.1 copy.30
  63.9 1.2 reduce.2
  65.1 3.7 %all_to_all.35 = s32[2,64,1]{1,2,0:T(1,128)S(1)} all-to-all(s32[2,64,1]{1,2,0:T(1,128)S(1)} %broadcast_in_dim.44), channel_id=1, replica_groups=mesh['row'=4,'col_0'=4,'col_1'=4,'col_2'=2] {'col_2'}, dimensions={0} | all-to-all | bytes 1024 | tf_op jit(solution)/shard_map/all_to_all | solution.py:14
  68.8 3.6 all-to-all-start.4
  73.1 1.8 compare_select_fusion.2
  74.9 10.1 %all-to-all-start.3 = ((s32[128,1,1]{2,1,0:T(1,128)}), s32[128,1,1]{2,1,0:T(1,128)S(1)}, u32[]{:S(2)}, u32[]{:S(2)}) async-start(s32[128,1,1]{2,1,0:T(1,128)} %compare_select_fusion.2), calls=%async_computation.3 | async-start | bytes 131072 | tf_op jit(solution)/shard_map/all_to_all | solution.py:125
  85.0 1.1 reduce_sum.54
  86.1 8.2 %all-to-all-done.3 = s32[128,1,1]{2,1,0:T(1,128)S(1)} async-done(((s32[128,1,1]{2,1,0:T(1,128)}), s32[128,1,1]{2,1,0:T(1,128)S(1)}, u32[]{:S(2)}, u32[]{:S(2)}) %all-to-all-start.3) | async-done | bytes 544 | tf_op jit(solution)/shard_map/all_to_all | solution.py:125
  94.3 5.1 %all-to-all-start.5 = ((bf16[64,8,512]{2,1,0:T(8,128)(2,1)}), bf16[64,8,512]{2,1,0:T(8,128)(2,1)S(1)}, u32[]{:S(2)}, u32[]{:S(2)}) async-start(bf16[64,8,512]{2,1,0:T(8,128)(2,1)} %reduce_sum.54), calls=%async_computation.5 | async-start | bytes 1048576 | tf_op jit(solution)/shard_map/all_to_all | solution.py:44
  100.1 11.4 %gather_fusion = bf16[128,128,512]{2,1,0:T(8,128)(2,1)} fusion(bf16[64,128,512]{2,1,0:T(8,128)(2,1)} %get-tuple-element.3, s32[1024]{0:T(1024)S(1)} %pad_clamp_fusion.1), kind=kCustom, calls=%fused_computation | custom fusion | bytes 33554944 | tf_op jit(solution)/shard_map/gather | solution.py:124
  111.5 1.0 all-to-all-done.5
  112.5 9.7 %all-to-all-start.2 = ((bf16[128,128,512]{2,1,0:T(8,128)(2,1)}), bf16[128,128,512]{2,1,0:T(8,128)(2,1)}, u32[]{:S(2)}, u32[]{:S(2)}) async-start(bf16[128,128,512]{2,1,0:T(8,128)(2,1)} %gather_fusion), calls=%async_computation.2 | async-start | bytes 33554432 | tf_op jit(solution)/shard_map/all_to_all | solution.py:124
  122.3 2.4 reduce.3
  124.8 0.7 convert_reduce_fusion.1
  125.5 226.7 %all-to-all-done.2 = bf16[128,128,512]{2,1,0:T(8,128)(2,1)} async-done(((bf16[128,128,512]{2,1,0:T(8,128)(2,1)}), bf16[128,128,512]{2,1,0:T(8,128)(2,1)}, u32[]{:S(2)}, u32[]{:S(2)}) %all-to-all-start.2) | async-done | bytes 16777248 | tf_op jit(solution)/shard_map/all_to_all | solution.py:124
  352.2 8.6 %gather_fusion.1 = bf16[32,128,512]{2,1,0:T(8,128)(2,1)} fusion(bf16[128,128,512]{2,1,0:T(8,128)(2,1)} %all-to-all-done.2, s32[1024]{0:T(1024)S(1)} %pad_clamp_fusion), kind=kCustom, calls=%fused_computation.1 | custom fusion | bytes 8388736 | tf_op jit(solution)/shard_map/gather | solution.py:127
  (27 shorter events, 3.4 us)
Async XLA Ops:
  0.6 29.3 %copy-start = (bf16[512,512]{1,0:T(8,128)(2,1)S(1)}, bf16[512,512]{1,0:T(8,128)(2,1)}, u32[]{:S(2)}) copy-start(bf16[512,512]{1,0:T(8,128)(2,1)} %param.18) | copy-start | bytes 1572868
  2.0 61.9 %all-to-all-start = ((s32[64,1,1]{2,1,0:T(1,128)}), s32[64,1,1]{2,1,0:T(1,128)S(1)}, u32[]{:S(2)}, u32[]{:S(2)}) async-start(s32[64,1,1]{2,1,0:T(1,128)} %broadcast_in_dim.43), calls=%async_computation | async-start | bytes 65536 | tf_op jit(solution)/shard_map/all_to_all | solution.py:14
  17.3 12.6 %copy-start.4 = (f32[512]{0:T(512)S(1)}, f32[512]{0:T(512)}, u32[]{:S(2)}) copy-start(f32[512]{0:T(512)} %param.19) | copy-start | bytes 6148
  30.0 10.3 %copy-start.2 = (bf16[512,512]{1,0:T(8,128)(2,1)S(1)}, bf16[512,512]{1,0:T(8,128)(2,1)}, u32[]{:S(2)}) copy-start(bf16[512,512]{1,0:T(8,128)(2,1)} %param.22) | copy-start | bytes 1572868
  30.0 10.3 %copy-start.3 = (bf16[512,512]{1,0:T(8,128)(2,1)S(1)}, bf16[512,512]{1,0:T(8,128)(2,1)}, u32[]{:S(2)}) copy-start(bf16[512,512]{1,0:T(8,128)(2,1)} %param.20) | copy-start | bytes 1572868
  30.0 10.3 %copy-start.5 = (f32[512]{0:T(512)S(1)}, f32[512]{0:T(512)}, u32[]{:S(2)}) copy-start(f32[512]{0:T(512)} %param.23) | copy-start | bytes 6148
  30.0 10.2 %copy-start.6 = (f32[512]{0:T(512)S(1)}, f32[512]{0:T(512)}, u32[]{:S(2)}) copy-start(f32[512]{0:T(512)} %param.21) | copy-start | bytes 6148
  68.8 6.0 %all-to-all-start.4 = ((bf16[2,64,8,512]{3,2,1,0:T(8,128)(2,1)}), bf16[2,64,8,512]{3,2,1,0:T(8,128)(2,1)S(1)}, u32[]{:S(2)}, u32[]{:S(2)}) async-start(bf16[2,64,8,512]{3,2,1,0:T(8,128)(2,1)} %bitcast.28), calls=%async_computation.4 | async-start | bytes 2097152 | tf_op jit(solution)/shard_map/all_to_all | solution.py:36
  74.9 19.4 %all-to-all-start.3 = ((s32[128,1,1]{2,1,0:T(1,128)}), s32[128,1,1]{2,1,0:T(1,128)S(1)}, u32[]{:S(2)}, u32[]{:S(2)}) async-start(s32[128,1,1]{2,1,0:T(1,128)} %compare_select_fusion.2), calls=%async_computation.3 | async-start | bytes 131072 | tf_op jit(solution)/shard_map/all_to_all | solution.py:125
  94.3 18.2 %all-to-all-start.5 = ((bf16[64,8,512]{2,1,0:T(8,128)(2,1)}), bf16[64,8,512]{2,1,0:T(8,128)(2,1)S(1)}, u32[]{:S(2)}, u32[]{:S(2)}) async-start(bf16[64,8,512]{2,1,0:T(8,128)(2,1)} %reduce_sum.54), calls=%async_computation.5 | async-start | bytes 1048576 | tf_op jit(solution)/shard_map/all_to_all | solution.py:44
  112.5 239.7 %all-to-all-start.2 = ((bf16[128,128,512]{2,1,0:T(8,128)(2,1)}), bf16[128,128,512]{2,1,0:T(8,128)(2,1)}, u32[]{:S(2)}, u32[]{:S(2)}) async-start(bf16[128,128,512]{2,1,0:T(8,128)(2,1)} %gather_fusion), calls=%async_computation.2 | async-start | bytes 33554432 | tf_op jit(solution)/shard_map/all_to_all | solution.py:124
  122.2 238.5 %copy-start.1 = (bf16[512,512]{1,0:T(8,128)(2,1)S(1)}, bf16[512,512]{1,0:T(8,128)(2,1)}, u32[]{:S(2)}) copy-start(bf16[512,512]{1,0:T(8,128)(2,1)} %param.18) | copy-start | bytes 1572868
where the time goes:
time: 368 us; the launch traced here: 361 us
  waiting for transfers between devices  236 us (64%)
  starting transfers between devices  40.1 us (11%)
  matrix products  37.1 us (10%)
  local copies, waits for them, and re-layouts  22.8 us (6%)
  other arithmetic  19 us (5%)
  blocking collectives  3.7 us (1%)
    all_to_all x1, waiting for transfers between devices, body(): lax.all_to_all(results[picked], ROW_COL, split_axis=0, concat_axis=0, til...  227 us
    dot_general x1, matrix products, perceptron(): jnp.dot(hidden_two, w_third, preferred_element_type=jnp.float32) + b_third  13.2 us
    dot_general x1, matrix products, blend_nodes(): jnp.einsum('gkl,glh->gkh', adjacency, features, preferred_element_type=jn...  12.6 us
    all_to_all x1, starting transfers between devices, sent_to_all(): return lax.all_to_all(copies, axis, split_axis=0, concat_axis=0, tiled=True)  11.5 us
    gather x1, local copies, waits for them, and re-layouts, body(): results[picked]  11.4 us
    dot_general x1, matrix products, perceptron(): jnp.dot(flat_rows, w_first, preferred_element_type=jnp.float32) + b_first  10.2 us
    all_to_all x1, starting transfers between devices, body(): lax.all_to_all(slot_tags, ROW_COL, split_axis=0, concat_axis=0, tiled=True)  10.1 us
    all_to_all x1, starting transfers between devices, body(): lax.all_to_all(results[picked], ROW_COL, split_axis=0, concat_axis=0, til...  9.73 us
  transfers between devices with their start and end apart: 5, of which 3 were waited for; matrix products, arithmetic and copies ran while one was open for 19% of the time, Pallas kernels for 0%

commit v1 on v0

v1 whole, which is shorter than its diff:
```python
import functools

import jax
import jax.numpy as jnp
from jax import lax
from jax.experimental import pallas as pl
from jax.experimental.pallas import tpu as pltpu
from jax.sharding import Mesh
from jax.sharding import PartitionSpec as P

G_DEV = 32
READ_DEV = 8
ROW_COL = ("row", "col_0", "col_1", "col_2")
CHIP = ("row", "col_0", "col_1")
SWAP = [(0, 1), (1, 0)]
PACK = 4
POOL = 8
MLP = 4


def masked_sum(keep, values, axis):
    return jnp.sum(jnp.where(keep, values, 0), axis=axis)


def blend_kernel(own_idx, par_idx, from_par, scale, *refs):
    owns, pars = refs[:PACK], refs[PACK : 2 * PACK]
    own_edges, par_edges, out = refs[2 * PACK :]
    step = pl.program_id(0)
    nodes = owns[0].shape[1]
    slots = own_edges.shape[-1]
    node_index = lax.broadcasted_iota(jnp.int32, (nodes, slots), 0)
    for lane in range(PACK):
        slot = step * PACK + lane
        pick = from_par[slot] == 1
        features = jnp.where(pick, pars[lane][0], owns[lane][0])
        edges = jnp.where(pick, par_edges[par_idx[slot]], own_edges[own_idx[slot]])
        sources = (node_index == edges[0:1, :]).astype(jnp.bfloat16)
        targets = (node_index == edges[1:2, :]).astype(jnp.bfloat16)
        adjacency = lax.dot_general(
            targets, sources, (((1,), (1,)), ((), ())), preferred_element_type=jnp.float32
        ).astype(jnp.bfloat16)
        neighbour = jnp.dot(adjacency, features, preferred_element_type=jnp.float32)
        out[lane] = (scale[0] * features.astype(jnp.float32) + neighbour).astype(jnp.bfloat16)


def blended_slots(own, par, own_edges, par_edges, own_idx, par_idx, from_par, scale):
    slots, nodes, hidden = own.shape
    count = own_idx.shape[0]

    def picked(table, lane):
        return pl.BlockSpec(
            (1, nodes, hidden), lambda i, *tables: (tables[table][i * PACK + lane], 0, 0)
        )

    whole = pl.BlockSpec(own_edges.shape, lambda i, *tables: (0, 0, 0))
    return pl.pallas_call(
        blend_kernel,
        out_shape=jax.ShapeDtypeStruct((count, nodes, hidden), jnp.bfloat16),
        grid_spec=pltpu.PrefetchScalarGridSpec(
            num_scalar_prefetch=4,
            grid=(count // PACK,),
            in_specs=[picked(0, lane) for lane in range(PACK)]
            + [picked(1, lane) for lane in range(PACK)]
            + [whole, whole],
            out_specs=pl.BlockSpec((PACK, nodes, hidden), lambda i, *tables: (i, 0, 0)),
        ),
        compiler_params=pltpu.CompilerParams(dimension_semantics=("arbitrary",)),
        cost_estimate=pl.CostEstimate(
            flops=2 * count * nodes * nodes * (own_edges.shape[-1] + hidden),
            bytes_accessed=4 * count * nodes * hidden,
            transcendentals=0,
        ),
        name="blend",
    )(own_idx, par_idx, from_par, scale, *[own] * PACK, *[par] * PACK, own_edges, par_edges)


def perceptron(rows, weights):
    w_first, b_first, w_second, b_second, w_third, b_third = weights
    for w, b in ((w_first, b_first), (w_second, b_second)):
        total = jnp.dot(rows, w[...], preferred_element_type=jnp.float32) + b[...]
        rows = jnp.maximum(total, 0.0).astype(jnp.bfloat16)
    return jnp.dot(rows, w_third[...], preferred_element_type=jnp.float32) + b_third[...]


def weight_specs(weights):
    return [pl.BlockSpec(w.shape, lambda i, *tables: (0, 0)) for w in weights]


def mlp_cost(rows, hidden):
    return pl.CostEstimate(
        flops=6 * rows * hidden * hidden, bytes_accessed=4 * rows * hidden, transcendentals=0
    )


def pool_kernel(counts, rows_ref, *refs):
    weights, out = refs[:6], refs[6]
    step = pl.program_id(0)
    many, nodes, hidden = rows_ref.shape
    result = perceptron(rows_ref[...].reshape(many * nodes, hidden), weights)
    node_index = lax.broadcasted_iota(jnp.int32, (nodes, 1), 0)
    for lane in range(many):
        count = counts[step * many + lane]
        part = result[lane * nodes : (lane + 1) * nodes]
        kept = jnp.where(node_index < count, part, 0.0).astype(jnp.bfloat16).astype(jnp.float32)
        shown = jnp.maximum(count, 1).astype(jnp.float32)
        out[lane : lane + 1, :] = jnp.sum(kept, axis=0, keepdims=True) / shown


def pooled_slots(blended, counts, weights):
    count, nodes, hidden = blended.shape
    return pl.pallas_call(
        pool_kernel,
        out_shape=jax.ShapeDtypeStruct((count, hidden), jnp.float32),
        grid_spec=pltpu.PrefetchScalarGridSpec(
            num_scalar_prefetch=1,
            grid=(count // POOL,),
            in_specs=[pl.BlockSpec((POOL, nodes, hidden), lambda i, *tables: (i, 0, 0))]
            + weight_specs(weights),
            out_specs=pl.BlockSpec((POOL, hidden), lambda i, *tables: (i, 0)),
        ),
        compiler_params=pltpu.CompilerParams(dimension_semantics=("arbitrary",)),
        cost_estimate=mlp_cost(count * nodes, hidden),
        name="pool",
    )(counts, blended, *weights)


def place_kernel(chips, counts, *refs):
    blocks, weights, out = refs[:MLP], refs[MLP : MLP + 6], refs[MLP + 6]
    step = pl.program_id(0)
    nodes = out.shape[1]
    rows = jnp.concatenate([block[0] for block in blocks], axis=0)
    result = perceptron(rows, weights)
    node_index = lax.broadcasted_iota(jnp.int32, (nodes, 1), 0)
    for lane in range(MLP):
        part = result[lane * nodes : (lane + 1) * nodes]
        live = node_index < counts[step * MLP + lane]
        out[lane] = jnp.where(live, part, 0.0).astype(jnp.bfloat16)


def placed_nodes(arrived, chips, counts, weights):
    _, nodes, hidden = arrived.shape

    def picked(lane):
        return pl.BlockSpec(
            (1, nodes, hidden), lambda i, *tables: (tables[0][i * MLP + lane], 0, 0)
        )

    return pl.pallas_call(
        place_kernel,
        out_shape=jax.ShapeDtypeStruct((G_DEV, nodes, hidden), jnp.bfloat16),
        grid_spec=pltpu.PrefetchScalarGridSpec(
            num_scalar_prefetch=2,
            grid=(G_DEV // MLP,),
            in_specs=[picked(lane) for lane in range(MLP)] + weight_specs(weights),
            out_specs=pl.BlockSpec((MLP, nodes, hidden), lambda i, *tables: (i, 0, 0)),
        ),
        compiler_params=pltpu.CompilerParams(dimension_semantics=("arbitrary",)),
        cost_estimate=mlp_cost(G_DEV * nodes, hidden),
        name="place",
    )(chips, counts, *[arrived] * MLP, *weights)


def sum_over_axis(blocks, axis):
    size = lax.axis_size(axis)
    me = lax.axis_index(axis)
    rounded = blocks.astype(jnp.bfloat16)
    total = lax.dynamic_index_in_dim(blocks, me, 0, keepdims=False).astype(jnp.float32)
    for shift in range(1, size):
        part = lax.dynamic_index_in_dim(rounded, (me + shift) % size, 0, keepdims=False)
        ring = [(i, (i + shift) % size) for i in range(size)]
        total = total + lax.ppermute(part, axis, ring).astype(jnp.float32)
    return total


def body(
    node_features,
    node_counts,
    edge_list,
    readout_ids,
    live_graphs,
    self_weight,
    w_first,
    b_first,
    w_second,
    b_second,
    w_third,
    b_third,
):
    weights = (
        w_first,
        b_first[None, :],
        w_second,
        b_second[None, :],
        w_third,
        b_third[None, :],
    )
    devices = lax.axis_size(ROW_COL)
    capacity, nodes, hidden = node_features.shape
    me = lax.axis_index(ROW_COL)
    core = lax.axis_index("col_2")
    chip = me // 2

    par_features = lax.ppermute(node_features, "col_2", SWAP)
    par_edges = lax.ppermute(edge_list, "col_2", SWAP)
    info = jnp.concatenate([live_graphs, node_counts, readout_ids])
    table = lax.all_to_all(
        jnp.broadcast_to(info[None], (devices, info.shape[0])), ROW_COL, 0, 0, tiled=True
    )
    live = table[:, 0]
    all_counts = table[:, 1 : 1 + capacity]

    device = lax.broadcasted_iota(jnp.int32, (devices,), 0)
    chip_offset = masked_sum(device < 2 * chip, live, 0)
    live_a = masked_sum(device == 2 * chip, live, 0)
    live_b = masked_sum(device == 2 * chip + 1, live, 0)
    slot = lax.broadcasted_iota(jnp.int32, (devices // 2,), 0)
    number = (2 * slot + core - chip_offset) % devices
    idx_a = jnp.clip(number, 0, live_a - 1)
    idx_b = jnp.clip(number - live_a, 0, live_b - 1)
    from_b = number >= live_a
    filled = number < live_a + live_b
    own_idx = jnp.where(core == 0, idx_a, idx_b)
    par_idx = jnp.where(core == 0, idx_b, idx_a)
    from_par = jnp.where(core == 0, from_b, ~from_b).astype(jnp.int32)

    blended = blended_slots(
        node_features, par_features, edge_list, par_edges, own_idx, par_idx, from_par, self_weight
    )
    arrived = lax.all_to_all(blended, CHIP, split_axis=0, concat_axis=0, tiled=True)

    pair = lax.dynamic_slice_in_dim(table, 2 * chip, 2, 0)
    picked = jnp.where(from_b, capacity + idx_b, idx_a)
    spot = lax.broadcasted_iota(jnp.int32, (devices // 2, 2 * capacity), 1) == picked[:, None]
    slot_counts = masked_sum(spot, pair[:, 1 : 1 + capacity].reshape(1, -1), 1)
    slot_ids = masked_sum(spot, pair[:, 1 + capacity :].reshape(1, -1), 1)
    slot_ids = jnp.where(filled, slot_ids, -1)
    pooled = pooled_slots(blended, slot_counts, weights)
    groups = READ_DEV * devices
    id_keys = lax.broadcasted_iota(jnp.int32, (groups, slot_ids.shape[0]), 0)
    members = (id_keys == slot_ids[None, :]).astype(jnp.float32)
    terms = jnp.dot(
        members, pooled, precision=lax.Precision.HIGHEST, preferred_element_type=jnp.float32
    )
    terms = terms.astype(jnp.bfloat16).reshape(devices // 2, 2, READ_DEV, hidden).swapaxes(0, 1)
    sums = sum_over_axis(terms, "col_2")
    sums = sums.reshape(devices // 8, 4, READ_DEV, hidden).swapaxes(0, 1)
    sums = sum_over_axis(sums, "col_1")
    sums = sums.reshape(devices // 32, 4, READ_DEV, hidden).swapaxes(0, 1)
    sums = sum_over_axis(sums, "col_0")
    readout = sum_over_axis(sums, "row")

    order = lax.broadcasted_iota(jnp.int32, (G_DEV, 1), 0) * devices + me
    upto = masked_sum(device[None, :] <= device[:, None], live[None, :], 1)
    passed = upto[None, :] <= order
    source = jnp.sum(passed.astype(jnp.int32), axis=1)
    start = jnp.max(jnp.where(passed, upto[None, :], 0), axis=1)
    source_idx = order[:, 0] - start
    hit = (device[None, :, None] == source[:, None, None]) & (
        lax.broadcasted_iota(jnp.int32, (1, 1, capacity), 2) == source_idx[:, None, None]
    )
    counts = jnp.sum(jnp.where(hit, all_counts[None], 0), axis=(1, 2))
    node_out = placed_nodes(arrived, source // 2, counts, weights)
    return (node_out, readout)


def solution(mesh):
    split = Mesh(
        mesh.devices.reshape(mesh.shape["row"], 4, 4, 2), ("row", "col_0", "col_1", "col_2")
    )
    return jax.shard_map(
        body,
        mesh=split,
        in_specs=(
            P(ROW_COL, None, None),
            P(ROW_COL),
            P(ROW_COL, None, None),
            P(ROW_COL),
            P(ROW_COL),
            P(),
            P(),
            P(),
            P(),
            P(),
            P(),
            P(),
        ),
        out_specs=(P(ROW_COL, None, None), P(ROW_COL, None)),
        check_vma=False,
    )
```

time: 368 us -> 209 us (0.57); the launches traced: 361 us -> 205 us
  waiting for transfers between devices: 236 us -> 93.2 us
  Pallas kernels: 0 us -> 48 us
  matrix products: 37.1 us -> 1.88 us
  local copies, waits for them, and re-layouts: 22.8 us -> 1.86 us
  other arithmetic: 19 us -> 9.22 us
  starting transfers between devices: 40.1 us -> 46.4 us
  blocking collectives: 3.7 us -> 0 us
    all_to_all x5 -> x2, waiting for transfers between devices: 236 us -> 8.6 us  [the longest x1 8.59 us: body(): lax.all_to_all(jnp.broadcast_to(info[None], (devices, info.shape[0])), RO...]
    ppermute x0 -> x12, waiting for transfers between devices: none -> 84.6 us  [the longest x10 84.6 us: sum_over_axis(): total = total + lax.ppermute(part, axis, ring).astype(jnp.float32)]
    pallas_call x0 -> x3, Pallas kernels: none -> 48 us  [the longest x1 18.4 us: pooled_slots(): pl.pallas_call(pool_kernel, out_shape=jax.ShapeDtypeStruct((count, hidden...]
    dot_general x4 -> x1, matrix products: 37.1 us -> 1.88 us  [body(): jnp.dot(members, pooled, precision=lax.Precision.HIGHEST, preferred_eleme...]
    ppermute x0 -> x12, starting transfers between devices: none -> 28.8 us  [the longest x10 28.6 us: sum_over_axis(): total = total + lax.ppermute(part, axis, ring).astype(jnp.float32)]
    all_to_all x5 -> x2, starting transfers between devices: 40.1 us -> 17.6 us  [the longest x1 11.3 us: body(): lax.all_to_all(jnp.broadcast_to(info[None], (devices, info.shape[0])), RO...]
    gather x2 -> x0, local copies, waits for them, and re-layouts: 20 us -> none  [the longest x1 11.4 us: body(): results[picked]]
    reduce_sum x5 -> x4, other arithmetic: 10.9 us -> 3.01 us  [the longest x1 1.55 us: body(): counts = jnp.sum(jnp.where(hit, all_counts[None], 0), axis=(1, 2))]
  transfers between devices with their start and end apart: 5 -> 14, of which waited for: 3 -> 7; matrix products, arithmetic and copies ran while one was open for 19% -> 6% of each run, Pallas kernels for 0% -> 9%
where the time goes in v1:
time: 209 us; the launch traced here: 205 us
  waiting for transfers between devices  93.2 us (45%)
  Pallas kernels  48 us (23%)
  starting transfers between devices  46.4 us (22%)
  other arithmetic  9.22 us (4%)
  between operations  4.88 us (2%)
    ppermute x10, waiting for transfers between devices, sum_over_axis(): total = total + lax.ppermute(part, axis, ring).astype(jnp.float32)  84.6 us
    ppermute x10, starting transfers between devices, sum_over_axis(): total = total + lax.ppermute(part, axis, ring).astype(jnp.float32)  28.6 us
    pallas_call x1, Pallas kernels, pooled_slots(): pl.pallas_call(pool_kernel, out_shape=jax.ShapeDtypeStruct((count, hidden...  18.4 us
    pallas_call x1, Pallas kernels, blended_slots(): pl.pallas_call(blend_kernel, out_shape=jax.ShapeDtypeStruct((count, nodes...  17.5 us
    pallas_call x1, Pallas kernels, placed_nodes(): pl.pallas_call(place_kernel, out_shape=jax.ShapeDtypeStruct((G_DEV, nodes...  12.1 us
    all_to_all x1, starting transfers between devices, body(): lax.all_to_all(jnp.broadcast_to(info[None], (devices, info.shape[0])), RO...  11.3 us
    all_to_all x1, waiting for transfers between devices, body(): lax.all_to_all(jnp.broadcast_to(info[None], (devices, info.shape[0])), RO...  8.59 us
    all_to_all x1, starting transfers between devices, body(): lax.all_to_all(blended, CHIP, split_axis=0, concat_axis=0, tiled=True)  6.36 us
  transfers between devices with their start and end apart: 14, of which 7 were waited for; matrix products, arithmetic and copies ran while one was open for 6% of the time, Pallas kernels for 9%

profile of v1, /device:TPU:0, one launch (start us, length us, event | category | flops | bytes accessed | tf_op | source)
XLA Modules:
  0.0 205.5 jit_solution(14325297729548428676)
XLA Ops:
  1.4 0.7 pad_add_fusion
  2.8 11.3 %all-to-all-start = ((s32[128,1,129]{2,1,0:T(1,128)}), s32[128,1,129]{2,1,0:T(1,128)S(1)}, u32[]{:S(2)}, u32[]{:S(2)}) async-start(s32[128,1,129]{2,1,0:T(1,128)} %broadcast_in_dim.93), calls=%async_computation | async-start | bytes 262144 | tf_op jit(solution)/shard_map/all_to_all | solution.py:206
  14.9 8.6 %all-to-all-done = s32[128,1,129]{2,1,0:T(1,128)S(1)} async-done(((s32[128,1,129]{2,1,0:T(1,128)}), s32[128,1,129]{2,1,0:T(1,128)S(1)}, u32[]{:S(2)}, u32[]{:S(2)}) %all-to-all-start) | async-done | bytes 66080 | tf_op jit(solution)/shard_map/all_to_all | solution.py:206
  27.1 1.2 compare_select_fusion.10
  29.1 1.2 compare_select_fusion.3
  30.3 1.2 fusion.9.from_par
  32.1 17.5 %blend.1.rows_ref = bf16[64,128,512]{2,1,0:T(8,128)(2,1)} custom-call(s32[64]{0:T(128)} %get-tuple-element.26.own_idx, s32[64]{0:T(128)} %get-tuple-element.25.par_idx, s32[64]{0:T(128)} %fusion.9.from_par, f32[1]{0:T(128)S(6)} %copy.39.scale, bf16[64,128,512]{2,1,0:T(8,128)(2,1)} %refs_3_.1, bf16[64,128,512]{2,1,0:T(8,128)(2,1)} %refs_3_.1, ...), custom_call_target="tpu_custom_call" | custom-call | flops 1610612736 | bytes 16777216 | tf_op jit(solution)/shard_map/blend/pallas_call | solution.py:56
  49.6 6.4 %all-to-all-start.1 = ((bf16[64,128,512]{2,1,0:T(8,128)(2,1)}), bf16[64,128,512]{2,1,0:T(8,128)(2,1)}, u32[]{:S(2)}, u32[]{:S(2)}) async-start(bf16[64,128,512]{2,1,0:T(8,128)(2,1)} %blend.1.rows_ref), calls=%async_computation.1 | async-start | bytes 16777216 | tf_op jit(solution)/shard_map/all_to_all | solution.py:229
  56.3 18.4 %pool.1 = f32[64,512]{1,0:T(8,128)} custom-call(s32[64]{0:T(128)} %get-tuple-element.8.counts, bf16[64,128,512]{2,1,0:T(8,128)(2,1)} %blend.1.rows_ref, bf16[512,512]{1,0:T(8,128)(2,1)} %refs_0_.3, f32[1,512]{1,0:T(1,128)} %bitcast.71, bf16[512,512]{1,0:T(8,128)(2,1)} %refs_2_.3, f32[1,512]{1,0:T(1,128)} %bitcast.73, bf16[512,512]{1,0:T(8,128)(2,1)} %refs_4_.3, ...), custom_call_target="tpu_custom_call" | custom-call | flops 12884901888 | bytes 16777216 | tf_op jit(solution)/shard_map/pool/pallas_call | solution.py:111
  74.7 1.9 convolution_convert_fusion
  77.0 1.6 collective-permute-done.2
  78.8 1.6 collective-permute-start.3
  80.4 2.7 %collective-permute-start.4 = (bf16[16,8,512]{2,1,0:T(8,128)(2,1)S(1)}, bf16[16,8,512]{2,1,0:T(8,128)(2,1)S(1)}, u32[]{:S(2)}, u32[]{:S(2)}) collective-permute-start(bf16[16,8,512]{2,1,0:T(8,128)(2,1)S(1)} %get-tuple-element.15), channel_id=1, source_target_pairs={{0,4},{2,6},{4,0},{6,2},{1,5},{3,7},{5,1},{7,3},{8,12},{10,14},{12... | collective-permute-start | bytes 393224 | tf_op jit(solution)/shard_map/ppermute | solution.py:171
  83.1 1.5 collective-permute-start.5
  84.6 74.8 %collective-permute-done.3 = bf16[16,8,512]{2,1,0:T(8,128)(2,1)S(1)} collective-permute-done((bf16[16,8,512]{2,1,0:T(8,128)(2,1)S(1)}, bf16[16,8,512]{2,1,0:T(8,128)(2,1)S(1)}, u32[]{:S(2)}, u32[]{:S(2)}) %collective-permute-start.3) | collective-permute-done | bytes 131104 | tf_op jit(solution)/shard_map/ppermute | solution.py:171
  159.4 4.8 %collective-permute-done.4 = bf16[16,8,512]{2,1,0:T(8,128)(2,1)S(1)} collective-permute-done((bf16[16,8,512]{2,1,0:T(8,128)(2,1)S(1)}, bf16[16,8,512]{2,1,0:T(8,128)(2,1)S(1)}, u32[]{:S(2)}, u32[]{:S(2)}) %collective-permute-start.4) | collective-permute-done | bytes 131104 | tf_op jit(solution)/shard_map/ppermute | solution.py:171
  164.4 14.4 %collective-permute-start.6 = (bf16[4,8,512]{2,1,0:T(8,128)(2,1)S(1)}, bf16[4,8,512]{2,1,0:T(8,128)(2,1)S(1)}, u32[]{:S(2)}, u32[]{:S(2)}) collective-permute-start(bf16[4,8,512]{2,1,0:T(8,128)(2,1)S(1)} %get-tuple-element.16), channel_id=1, source_target_pairs={{0,8},{8,16},{16,24},{24,0},{1,9},{9,17},{17,25},{25,1},{2,10},{10... | collective-permute-start | bytes 98312 | tf_op jit(solution)/shard_map/ppermute | solution.py:171
  178.8 2.8 %collective-permute-start.8 = (bf16[4,8,512]{2,1,0:T(8,128)(2,1)S(1)}, bf16[4,8,512]{2,1,0:T(8,128)(2,1)S(1)}, u32[]{:S(2)}, u32[]{:S(2)}) collective-permute-start(bf16[4,8,512]{2,1,0:T(8,128)(2,1)S(1)} %get-tuple-element.17), channel_id=1, source_target_pairs={{0,24},{8,0},{16,8},{24,16},{1,25},{9,1},{17,9},{25,17},{2,26},{10... | collective-permute-start | bytes 98312 | tf_op jit(solution)/shard_map/ppermute | solution.py:171
  182.1 2.0 collective-permute-done.7
  184.2 3.6 %collective-permute-start.10 = (bf16[8,512]{1,0:T(8,128)(2,1)S(1)}, bf16[8,512]{1,0:T(8,128)(2,1)S(1)}, u32[]{:S(2)}, u32[]{:S(2)}) collective-permute-start(bf16[8,512]{1,0:T(8,128)(2,1)S(1)} %get-tuple-element.21), channel_id=1, source_target_pairs={{0,64},{32,96},{64,0},{96,32},{1,65},{33,97},{65,1},{97,33},{2,66}... | collective-permute-start | bytes 24584 | tf_op jit(solution)/shard_map/ppermute | solution.py:171
  187.9 2.0 collective-permute-start.9
  189.9 1.5 select_reduce_fusion.counts
  191.5 1.2 collective-permute-done.9
  193.3 12.1 %place.1 = bf16[32,128,512]{2,1,0:T(8,128)(2,1)} custom-call(s32[32]{0:T(128)} %and_select_fusion.1.chips, s32[32]{0:T(128)} %select_reduce_fusion.counts, bf16[64,128,512]{2,1,0:T(8,128)(2,1)} %all-to-all-done.1.refs_0_.refs_1_.refs_2_.refs_3_, bf16[64,128,512]{2,1,0:T(8,128)(2,1)} %all-to-all-done.1.refs_0_.refs_1_.refs_2_.refs_3_, ...), custom_call_target="tpu_custom_call" | custom-call | flops 6442450944 | bytes 8388608 | tf_op jit(solution)/shard_map/place/pallas_call | solution.py:148
  (42 shorter events, 5.5 us)
Async XLA Ops:
  0.6 30.9 %collective-permute-start = (bf16[64,128,512]{2,1,0:T(8,128)(2,1)}, bf16[64,128,512]{2,1,0:T(8,128)(2,1)}, u32[]{:S(2)}, u32[]{:S(2)}) collective-permute-start(bf16[64,128,512]{2,1,0:T(8,128)(2,1)} %refs_3_.1), channel_id=1, source_target_pairs={{0,1},{1,0},{2,3},{3,2},{4,5},{5,4},{6,7},{7,6},{8,9},{9,8},{10,11... | collective-permute-start | bytes 25165832 | tf_op jit(solution)/shard_map/ppermute | solution.py:203
  2.8 20.7 %all-to-all-start = ((s32[128,1,129]{2,1,0:T(1,128)}), s32[128,1,129]{2,1,0:T(1,128)S(1)}, u32[]{:S(2)}, u32[]{:S(2)}) async-start(s32[128,1,129]{2,1,0:T(1,128)} %broadcast_in_dim.93), calls=%async_computation | async-start | bytes 262144 | tf_op jit(solution)/shard_map/all_to_all | solution.py:206
  14.1 17.3 %collective-permute-start.1 = (s32[64,2,256]{2,1,0:T(2,128)}, s32[64,2,256]{2,1,0:T(2,128)S(1)}, u32[]{:S(2)}, u32[]{:S(2)}) collective-permute-start(s32[64,2,256]{2,1,0:T(2,128)} %refs_8_.2), channel_id=1, source_target_pairs={{0,1},{1,0},{2,3},{3,2},{4,5},{5,4},{6,7},{7,6},{8,9},{9,8},{10,11... | collective-permute-start | bytes 393224 | tf_op jit(solution)/shard_map/ppermute | solution.py:204
  31.5 0.7 copy-start
  49.6 143.7 %all-to-all-start.1 = ((bf16[64,128,512]{2,1,0:T(8,128)(2,1)}), bf16[64,128,512]{2,1,0:T(8,128)(2,1)}, u32[]{:S(2)}, u32[]{:S(2)}) async-start(bf16[64,128,512]{2,1,0:T(8,128)(2,1)} %blend.1.rows_ref), calls=%async_computation.1 | async-start | bytes 16777216 | tf_op jit(solution)/shard_map/all_to_all | solution.py:229
  76.6 2.0 collective-permute-start.2
  78.8 80.6 %collective-permute-start.3 = (bf16[16,8,512]{2,1,0:T(8,128)(2,1)S(1)}, bf16[16,8,512]{2,1,0:T(8,128)(2,1)S(1)}, u32[]{:S(2)}, u32[]{:S(2)}) collective-permute-start(bf16[16,8,512]{2,1,0:T(8,128)(2,1)S(1)} %get-tuple-element.13), channel_id=1, source_target_pairs={{0,2},{2,4},{4,6},{6,0},{1,3},{3,5},{5,7},{7,1},{8,10},{10,12},{12... | collective-permute-start | bytes 393224 | tf_op jit(solution)/shard_map/ppermute | solution.py:171
  80.4 83.8 %collective-permute-start.4 = (bf16[16,8,512]{2,1,0:T(8,128)(2,1)S(1)}, bf16[16,8,512]{2,1,0:T(8,128)(2,1)S(1)}, u32[]{:S(2)}, u32[]{:S(2)}) collective-permute-start(bf16[16,8,512]{2,1,0:T(8,128)(2,1)S(1)} %get-tuple-element.15), channel_id=1, source_target_pairs={{0,4},{2,6},{4,0},{6,2},{1,5},{3,7},{5,1},{7,3},{8,12},{10,14},{12... | collective-permute-start | bytes 393224 | tf_op jit(solution)/shard_map/ppermute | solution.py:171
  83.1 81.2 %collective-permute-start.5 = (bf16[16,8,512]{2,1,0:T(8,128)(2,1)S(1)}, bf16[16,8,512]{2,1,0:T(8,128)(2,1)S(1)}, u32[]{:S(2)}, u32[]{:S(2)}) collective-permute-start(bf16[16,8,512]{2,1,0:T(8,128)(2,1)S(1)} %get-tuple-element.14), channel_id=1, source_target_pairs={{0,6},{2,0},{4,2},{6,4},{1,7},{3,1},{5,3},{7,5},{8,14},{10,8},{12,... | collective-permute-start | bytes 393224 | tf_op jit(solution)/shard_map/ppermute | solution.py:171
  164.4 17.8 %collective-permute-start.6 = (bf16[4,8,512]{2,1,0:T(8,128)(2,1)S(1)}, bf16[4,8,512]{2,1,0:T(8,128)(2,1)S(1)}, u32[]{:S(2)}, u32[]{:S(2)}) collective-permute-start(bf16[4,8,512]{2,1,0:T(8,128)(2,1)S(1)} %get-tuple-element.16), channel_id=1, source_target_pairs={{0,8},{8,16},{16,24},{24,0},{1,9},{9,17},{17,25},{25,1},{2,10},{10... | collective-permute-start | bytes 98312 | tf_op jit(solution)/shard_map/ppermute | solution.py:171
  178.8 5.4 %collective-permute-start.7 = (bf16[4,8,512]{2,1,0:T(8,128)(2,1)S(1)}, bf16[4,8,512]{2,1,0:T(8,128)(2,1)S(1)}, u32[]{:S(2)}, u32[]{:S(2)}) collective-permute-start(bf16[4,8,512]{2,1,0:T(8,128)(2,1)S(1)} %get-tuple-element.18), channel_id=1, source_target_pairs={{0,16},{8,24},{16,0},{24,8},{1,17},{9,25},{17,1},{25,9},{2,18},{10... | collective-permute-start | bytes 98312 | tf_op jit(solution)/shard_map/ppermute | solution.py:171
  178.8 5.4 %collective-permute-start.8 = (bf16[4,8,512]{2,1,0:T(8,128)(2,1)S(1)}, bf16[4,8,512]{2,1,0:T(8,128)(2,1)S(1)}, u32[]{:S(2)}, u32[]{:S(2)}) collective-permute-start(bf16[4,8,512]{2,1,0:T(8,128)(2,1)S(1)} %get-tuple-element.17), channel_id=1, source_target_pairs={{0,24},{8,0},{16,8},{24,16},{1,25},{9,1},{17,9},{25,17},{2,26},{10... | collective-permute-start | bytes 98312 | tf_op jit(solution)/shard_map/ppermute | solution.py:171
  184.2 7.2 %collective-permute-start.10 = (bf16[8,512]{1,0:T(8,128)(2,1)S(1)}, bf16[8,512]{1,0:T(8,128)(2,1)S(1)}, u32[]{:S(2)}, u32[]{:S(2)}) collective-permute-start(bf16[8,512]{1,0:T(8,128)(2,1)S(1)} %get-tuple-element.21), channel_id=1, source_target_pairs={{0,64},{32,96},{64,0},{96,32},{1,65},{33,97},{65,1},{97,33},{2,66}... | collective-permute-start | bytes 24584 | tf_op jit(solution)/shard_map/ppermute | solution.py:171
  187.9 3.7 %collective-permute-start.11 = (bf16[8,512]{1,0:T(8,128)(2,1)S(1)}, bf16[8,512]{1,0:T(8,128)(2,1)S(1)}, u32[]{:S(2)}, u32[]{:S(2)}) collective-permute-start(bf16[8,512]{1,0:T(8,128)(2,1)S(1)} %get-tuple-element.20), channel_id=1, source_target_pairs={{0,96},{32,0},{64,32},{96,64},{1,97},{33,1},{65,33},{97,65},{2,98}... | collective-permute-start | bytes 24584 | tf_op jit(solution)/shard_map/ppermute | solution.py:171
  187.9 4.9 %collective-permute-start.9 = (bf16[8,512]{1,0:T(8,128)(2,1)S(1)}, bf16[8,512]{1,0:T(8,128)(2,1)S(1)}, u32[]{:S(2)}, u32[]{:S(2)}) collective-permute-start(bf16[8,512]{1,0:T(8,128)(2,1)S(1)} %get-tuple-element.19), channel_id=1, source_target_pairs={{0,32},{32,64},{64,96},{96,0},{1,33},{33,65},{65,97},{97,1},{2,34}... | collective-permute-start | bytes 24584 | tf_op jit(solution)/shard_map/ppermute | solution.py:171
